TPU v7x, 256 devices: a whole 4x4x8 slice. The times are simulated.
256 devices in a mesh: gy: 8 (over y, x_hi), gx: 32 (over x_lo, z, core).
Axes of the slice: x: 4 (x_hi: 2, x_lo: 2; x = x_hi * 2 + x_lo), y: 4, z: 8, core: 2. Of those that a mesh axis runs over, the one named last changes fastest.
Arguments:
- u_field: float32 [8, 2048, 2048], P(None, 'gx', 'gy')
- v_field: float32 [8, 2048, 2048], P(None, 'gx', 'gy')
- w_field: float32 [8, 2048, 2048], P(None, 'gx', 'gy')
- sep_x: int32 [16], replicated, may hold values from 1 to 128, as said below
- sep_y: int32 [16], replicated, may hold values from 1 to 256, as said below
- sep_z: int32 [16], replicated, may hold values from 1 to 4
Outputs:
- correlation: float32 [3, 16], replicated
Inputs may be any that keep to these rules, and one draw needn't show every extreme that they name: `sep_x`: every separation along x lies in 1 to 128, and 128 is among them in every draw; repeats may occur. `sep_y`: every separation along y lies in 1 to 256, and 256 is among them in every draw; repeats may occur.
All inputs are finite; a program needn't handle non-finite values.
Results may differ from a plain program's by a relative error of at most 0.0003.
Values sent between devices are 32-bit elements; how exact they have to be, the bound alone decides.
A program may use at most 64 MiB of HBM per device.

v0:
```python
import jax
import jax.numpy as jnp
from jax import lax
from jax.sharding import Mesh
from jax.sharding import PartitionSpec as P

GX = ("gx_0", "gx_1", "gx_2")
GY = ("gy_0", "gy_1")
GY_GX = ("gy_0", "gy_1", "gx_0", "gx_1", "gx_2")


def from_behind(value, axis, steps):
    count = lax.axis_size(axis)
    pairs = [(source, (source + steps) % count) for source in range(count)]
    return lax.ppermute(value, axis, pairs)


def by_axis(x, axes):
    for axis in axes:
        x = lax.psum(x, axis)
    return x


def lag_sums(widened, leading, lag_values, length, axis_dim):

    def one_lag(lag_entry):
        offset, lag_value = lag_entry
        head = lax.dynamic_slice_in_dim(widened, offset, length, axis_dim)
        tail = lax.dynamic_slice_in_dim(widened, offset + lag_value, length, axis_dim)
        return jnp.sum(head * tail)

    return lax.map(one_lag, (leading, lag_values))


def local(u_field, v_field, w_field, sep_x, sep_y, sep_z):
    planes, width_x, width_y = u_field.shape
    u_next = from_behind(u_field, GX, -1)
    u_after = from_behind(u_next, GX, -1)
    wide_x = jnp.concatenate([u_field, u_next, u_after], axis=1)
    v_next = from_behind(v_field, GY, -1)
    wide_y = jnp.concatenate([v_field, v_next], axis=2)
    offset_x = jnp.zeros_like(sep_x)
    offset_y = jnp.zeros_like(sep_y)
    sums_x = lag_sums(wide_x, offset_x, sep_x, width_x, 1)
    sums_y = lag_sums(wide_y, offset_y, sep_y, width_y, 2)
    padded = jnp.concatenate([w_field, jnp.zeros_like(w_field)], axis=0)

    def along_z(lag_value):
        shifted = lax.dynamic_slice_in_dim(padded, lag_value, planes, 0)
        return jnp.sum(w_field * shifted)

    sums_z = lax.map(along_z, sep_z)
    products = jnp.stack([sums_x, sums_y, sums_z], axis=0)
    squares = jnp.stack(
        [jnp.sum(u_field * u_field), jnp.sum(v_field * v_field), jnp.sum(w_field * w_field)]
    )
    totals, energy = (by_axis(products, GY_GX), by_axis(squares, GY_GX))
    factor = jnp.float32(planes) / (jnp.float32(planes) - sep_z.astype(jnp.float32))
    row_x = totals[0] / energy[0]
    row_y = totals[1] / energy[1]
    row_z = totals[2] / energy[2] * factor
    return jnp.stack([row_x, row_y, row_z], axis=0)


def solution(mesh):
    finer = Mesh(mesh.devices.reshape(4, 2, 2, 8, 2), ("gy_0", "gy_1", "gx_0", "gx_1", "gx_2"))
    placed = (P(None, GX, GY), P(None, GX, GY), P(None, GX, GY), P(), P(), P())
    return jax.shard_map(local, mesh=finer, in_specs=placed, out_specs=P(), check_vma=False)
```

profile of v0, /device:TPU:1, one launch (start us, length us, event | category | flops | bytes accessed | tf_op | source)
XLA Modules:
  0.0 266.0 jit_solution(17516855033638149033)
XLA Ops:
  0.0 3.2 %collective-permute-start = (f32[8,64,256]{2,1,0:T(8,128)}, f32[8,64,256]{2,1,0:T(8,128)S(1)}, u32[]{:S(2)}, u32[]{:S(2)}) collective-permute-start(f32[8,64,256]{2,1,0:T(8,128)} %param.12), channel_id=1, source_target_pairs={{0,31},{1,0},{2,1},{3,2},{4,3},{5,4},{6,5},{7,6},{8,7},{9,8},{10,9... | collective-permute-start | bytes 1572872 | tf_op jit(solution)/shard_map/ppermute | solution.py:15
  3.2 3.5 %collective-permute-start.2 = (f32[8,64,256]{2,1,0:T(8,128)}, f32[8,64,256]{2,1,0:T(8,128)}, u32[]{:S(2)}, u32[]{:S(2)}) collective-permute-start(f32[8,64,256]{2,1,0:T(8,128)} %param.13), channel_id=1, source_target_pairs={{0,224},{32,0},{64,32},{96,64},{128,96},{160,128},{192,160},{224,1... | collective-permute-start | bytes 1572872 | tf_op jit(solution)/shard_map/ppermute | solution.py:15
  6.7 1.1 concatenate.11
  7.9 69.8 %while.32 = (s32[]{:T(128)}, f32[16]{0:T(128)S(1)}, s32[16]{0:T(128)S(1)}, f32[16,64,256]{2,1,0:T(8,128)S(1)}, f32[8,64,256]{2,1,0:T(8,128)S(1)}, /*index=5*/s32[]{:T(128)}, s32[]{:T(128)}, s32[]{:T(128)}) while((s32[]{:T(128)}, f32[16]{0:T(128)S(1)}, s32[16]{0:T(128)S(1)}, f32[16,64,256]{2,1,0:T(8,128)S(1)}, f32[8,64,256]{2,1,0:T(8,128)S(1)}, ...), condition=%wide.region_8.9_spmd, body=%wide.region_6.8_spmd.sunk | while | flops 262148 | bytes 1048727 | solution.py:52
  80.1 2.0 pad_maximum_fusion.4
  82.0 6.2 %collective-permute-start.1 = (f32[8,64,256]{2,1,0:T(8,128)S(1)}, f32[8,64,256]{2,1,0:T(8,128)}, u32[]{:S(2)}, u32[]{:S(2)}) collective-permute-start(f32[8,64,256]{2,1,0:T(8,128)S(1)} %collective-permute-done), channel_id=1, source_target_pairs={{0,31},{1,0},{2,1},{3,2},{4,3},{5,4},{6,5},{7,6},{8,7},{9,8},{10,9... | collective-permute-start | bytes 1572872 | tf_op jit(solution)/shard_map/ppermute | solution.py:15
  88.3 1.2 pad_maximum_fusion.1
  89.5 70.9 %while.31 = (s32[]{:T(128)}, f32[16]{0:T(128)S(1)}, f32[8,64,512]{2,1,0:T(8,128)S(1)}, s32[16]{0:T(128)S(1)}, s32[]{:T(128)}, /*index=5*/s32[]{:T(128)}, s32[]{:T(128)}) while((s32[]{:T(128)}, f32[16]{0:T(128)S(1)}, f32[8,64,512]{2,1,0:T(8,128)S(1)}, s32[16]{0:T(128)S(1)}, s32[]{:T(128)}, /*index=5*/s32[]{:T(128)}, s32[]{:T(128)}) %tuple.58), condition=%wide.region_5.6_spmd, body=%wide.region_3.5_spmd.sunk | while | flops 262148 | bytes 1048719 | solution.py:32
  92.2 0.9 multiply_reduce_fusion.10
  96.6 0.9 multiply_reduce_fusion.10
  101.1 0.9 multiply_reduce_fusion.10
  105.5 0.9 multiply_reduce_fusion.10
  109.9 0.9 multiply_reduce_fusion.10
  114.3 0.9 multiply_reduce_fusion.10
  118.8 0.9 multiply_reduce_fusion.10
  123.2 0.9 multiply_reduce_fusion.10
  127.6 0.9 multiply_reduce_fusion.10
  132.1 0.9 multiply_reduce_fusion.10
  136.5 0.9 multiply_reduce_fusion.10
  140.9 0.9 multiply_reduce_fusion.10
  145.3 0.9 multiply_reduce_fusion.10
  149.8 0.9 multiply_reduce_fusion.10
  154.2 0.9 multiply_reduce_fusion.10
  158.6 0.9 multiply_reduce_fusion.10
  160.3 1.2 pad_maximum_fusion
  161.5 64.5 %while.30 = (s32[]{:T(128)}, f32[16]{0:T(128)S(1)}, f32[8,192,256]{2,1,0:T(8,128)S(1)}, s32[16]{0:T(128)S(1)}, s32[]{:T(128)}, /*index=5*/s32[]{:T(128)}, s32[]{:T(128)}) while((s32[]{:T(128)}, f32[16]{0:T(128)S(1)}, f32[8,192,256]{2,1,0:T(8,128)S(1)}, s32[16]{0:T(128)S(1)}, s32[]{:T(128)}, /*index=5*/s32[]{:T(128)}, s32[]{:T(128)}) %tuple.59), condition=%wide.region_2.3_spmd, body=%wide.region_0.2_spmd.sunk | while | flops 262148 | bytes 1048719 | solution.py:32
  226.0 6.5 %all-reduce.2 = (f32[3,16]{1,0:T(4,128)S(1)}, f32[3]{0:T(128)S(1)}) all-reduce(f32[3,16]{1,0:T(4,128)S(1)} %pad_maximum_fusion.2, f32[3]{0:T(128)S(1)} %pad_maximum_fusion.4), channel_id=1, replica_groups=mesh['gy_0'=4,'gy_1'=2,'gx_0'=2,'gx_1'=8,'gx_2'=2] {'gy_0'}, use_global_device_ids=true, to_apply=%region_9.10 | all-reduce | flops 51 | bytes 408 | tf_op jit(solution)/shard_map/psum | solution.py:20
  232.5 5.3 %all-reduce.5 = (f32[3,16]{1,0:T(4,128)S(1)}, f32[3]{0:T(128)S(1)}) all-reduce(f32[3,16]{1,0:T(4,128)S(1)} %get-tuple-element.107, f32[3]{0:T(128)S(1)} %get-tuple-element.108), channel_id=1, replica_groups=mesh['gy_0'=4,'gy_1'=2,'gx_0'=2,'gx_1'=8,'gx_2'=2] {'gy_1'}, use_global_device_ids=true, to_apply=%region_10.11 | all-reduce | flops 51 | bytes 408 | tf_op jit(solution)/shard_map/psum | solution.py:20
  237.8 3.8 %all-reduce.4 = (f32[3,16]{1,0:T(4,128)S(1)}, f32[3]{0:T(128)S(1)}) all-reduce(f32[3,16]{1,0:T(4,128)S(1)} %get-tuple-element.113, f32[3]{0:T(128)S(1)} %get-tuple-element.114), channel_id=1, replica_groups=mesh['gy_0'=4,'gy_1'=2,'gx_0'=2,'gx_1'=8,'gx_2'=2] {'gx_0'}, use_global_device_ids=true, to_apply=%region_11.12 | all-reduce | flops 51 | bytes 408 | tf_op jit(solution)/shard_map/psum | solution.py:20
  241.5 10.7 %all-reduce.1 = (f32[3,16]{1,0:T(4,128)S(1)}, f32[3]{0:T(128)S(1)}) all-reduce(f32[3,16]{1,0:T(4,128)S(1)} %get-tuple-element.111, f32[3]{0:T(128)S(1)} %get-tuple-element.112), channel_id=1, replica_groups=mesh['gy_0'=4,'gy_1'=2,'gx_0'=2,'gx_1'=8,'gx_2'=2] {'gx_1'}, use_global_device_ids=true, to_apply=%region_12.13 | all-reduce | flops 51 | bytes 408 | tf_op jit(solution)/shard_map/psum | solution.py:20
  252.3 10.6 %all-reduce.3 = (f32[3,16]{1,0:T(4,128)S(1)}, f32[3]{0:T(128)S(1)}) all-reduce(f32[3,16]{1,0:T(4,128)S(1)} %get-tuple-element.105, f32[3]{0:T(128)S(1)} %get-tuple-element.106), channel_id=1, replica_groups=mesh['gy_0'=4,'gy_1'=2,'gx_0'=2,'gx_1'=8,'gx_2'=2] {'gx_2'}, use_global_device_ids=true, to_apply=%region_13.14 | all-reduce | flops 51 | bytes 408 | tf_op jit(solution)/shard_map/psum | solution.py:20
  264.2 1.2 slice_divide_fusion.1
  (153 shorter events, 97.7 us)
Async XLA Ops:
  0.0 7.8 %copy-start = (f32[8,64,256]{2,1,0:T(8,128)S(1)}, f32[8,64,256]{2,1,0:T(8,128)}, u32[]{:S(2)}) copy-start(f32[8,64,256]{2,1,0:T(8,128)} %param.14) | copy-start | bytes 1572868
  0.0 7.8 %copy-start.3 = (s32[16]{0:T(128)S(1)}, s32[16]{0:T(128)}, u32[]{:S(2)}) copy-start(s32[16]{0:T(128)} %param.17) | copy-start | bytes 196
  0.0 82.0 %collective-permute-start = (f32[8,64,256]{2,1,0:T(8,128)}, f32[8,64,256]{2,1,0:T(8,128)S(1)}, u32[]{:S(2)}, u32[]{:S(2)}) collective-permute-start(f32[8,64,256]{2,1,0:T(8,128)} %param.12), channel_id=1, source_target_pairs={{0,31},{1,0},{2,1},{3,2},{4,3},{5,4},{6,5},{7,6},{8,7},{9,8},{10,9... | collective-permute-start | bytes 1572872 | tf_op jit(solution)/shard_map/ppermute | solution.py:15
  3.2 85.1 %collective-permute-start.2 = (f32[8,64,256]{2,1,0:T(8,128)}, f32[8,64,256]{2,1,0:T(8,128)}, u32[]{:S(2)}, u32[]{:S(2)}) collective-permute-start(f32[8,64,256]{2,1,0:T(8,128)} %param.13), channel_id=1, source_target_pairs={{0,224},{32,0},{64,32},{96,64},{128,96},{160,128},{192,160},{224,1... | collective-permute-start | bytes 1572872 | tf_op jit(solution)/shard_map/ppermute | solution.py:15
  7.9 69.9 %copy-start.1 = (f32[8,64,256]{2,1,0:T(8,128)S(1)}, f32[8,64,256]{2,1,0:T(8,128)}, u32[]{:S(2)}) copy-start(f32[8,64,256]{2,1,0:T(8,128)} %param.13) | copy-start | bytes 1572868
  7.9 71.4 %copy-start.2 = (f32[8,64,256]{2,1,0:T(8,128)S(1)}, f32[8,64,256]{2,1,0:T(8,128)}, u32[]{:S(2)}) copy-start(f32[8,64,256]{2,1,0:T(8,128)} %param.12) | copy-start | bytes 1572868
  78.4 11.0 %copy-start.4 = (s32[16]{0:T(128)S(1)}, s32[16]{0:T(128)}, u32[]{:S(2)}) copy-start(s32[16]{0:T(128)} %param.16) | copy-start | bytes 196
  82.0 78.3 %collective-permute-start.1 = (f32[8,64,256]{2,1,0:T(8,128)S(1)}, f32[8,64,256]{2,1,0:T(8,128)}, u32[]{:S(2)}, u32[]{:S(2)}) collective-permute-start(f32[8,64,256]{2,1,0:T(8,128)S(1)} %collective-permute-done), channel_id=1, source_target_pairs={{0,31},{1,0},{2,1},{3,2},{4,3},{5,4},{6,5},{7,6},{8,7},{9,8},{10,9... | collective-permute-start | bytes 1572872 | tf_op jit(solution)/shard_map/ppermute | solution.py:15
  160.3 1.2 copy-start.5
where the time goes:
time: 268 us; the launch traced here: 266 us
  loops' own time  97.6 us (36%)
  local copies, waits for them, and re-layouts  70.1 us (26%)
  other arithmetic  48.5 us (18%)
  blocking collectives  36.8 us (14%)
  starting transfers between devices  12.9 us (5%)
    another operation x2, loops' own time, lag_sums(): return lax.map(one_lag, (leading, lag_values))  64.4 us
    dynamic_update_slice x48, local copies, waits for them, and re-layouts, lag_sums(): return lax.map(one_lag, (leading, lag_values))  37.7 us
    psum x5, blocking collectives, by_axis(): x = lax.psum(x, axis)  36.8 us
    another operation x1, loops' own time, local(): sums_z = lax.map(along_z, sep_z)  33.3 us
    dynamic_slice x48, local copies, waits for them, and re-layouts, lag_sums(): return lax.map(one_lag, (leading, lag_values))  30.6 us
    reduce_sum x32, other arithmetic, one_lag(): return jnp.sum(head * tail)  26.2 us
    reduce_sum x16, other arithmetic, along_z(): return jnp.sum(w_field * shifted)  13.1 us
    ppermute x3, starting transfers between devices, from_behind(): return lax.ppermute(value, axis, pairs)  12.9 us
  transfers between devices with their start and end apart: 3, of which 0 were waited for; matrix products, arithmetic and copies ran while one was open for 30% of the time, Pallas kernels for 0%

commit v1 on v0

--- a/solution.py
+++ b/solution.py
@@ -9,6 +9,12 @@
 GY_GX = ("gy_0", "gy_1", "gx_0", "gx_1", "gx_2")
 
 
+def gather_and_add(array, name):
+    blocks = lax.all_gather(array, name, axis=0, tiled=False)
+    total = blocks.sum(axis=0)
+    return total
+
+
 def from_behind(value, axis, steps):
     count = lax.axis_size(axis)
     pairs = [(source, (source + steps) % count) for source in range(count)]
@@ -17,7 +23,7 @@
 
 def by_axis(x, axes):
     for axis in axes:
-        x = lax.psum(x, axis)
+        x = gather_and_add(x, axis)
     return x
 
 

time: 268 us -> 313 us (1.17)
  blocking collectives: 36.8 us -> 87.3 us
  loops' own time: 97.6 us -> 91.2 us
  starting transfers between devices: 12.9 us -> 7.11 us
  between operations: 0.12 us -> 3.44 us
    all_gather x0 -> x5, blocking collectives: none -> 44.6 us  [gather_and_add(): blocks = lax.all_gather(array, name, axis=0, tiled=False)]
    unnamed x0 -> x5, blocking collectives: none -> 42.7 us
    psum x5 -> x0, blocking collectives: 36.8 us -> none  [by_axis(): x = lax.psum(x, axis)]
    another operation x2, loops' own time: 64.4 us -> 58 us  [lag_sums(): return lax.map(one_lag, (leading, lag_values))]
    ppermute x3, starting transfers between devices: 12.9 us -> 7.11 us  [from_behind(): return lax.ppermute(value, axis, pairs)]
    unnamed x12 -> x36, local copies, waits for them, and re-layouts: 0.03 us -> 3.94 us
  transfers between devices with their start and end apart: 3 -> 3, of which waited for: 0 -> 0; matrix products, arithmetic and copies ran while one was open for 30% -> 27% of each run, Pallas kernels for 0% -> 0%
where the time goes in v1:
time: 313 us; the launch traced here: 308 us
  loops' own time  91.2 us (29%)
  blocking collectives  87.3 us (28%)
  local copies, waits for them, and re-layouts  69.8 us (22%)
  other arithmetic  49.4 us (16%)
  starting transfers between devices  7.11 us (2%)
  between operations  3.44 us (1%)
    another operation x2, loops' own time, lag_sums(): return lax.map(one_lag, (leading, lag_values))  58 us
    all_gather x5, blocking collectives, gather_and_add(): blocks = lax.all_gather(array, name, axis=0, tiled=False)  44.6 us
    unnamed x5, blocking collectives  42.7 us
    dynamic_update_slice x48, local copies, waits for them, and re-layouts, lag_sums(): return lax.map(one_lag, (leading, lag_values))  35.6 us
    another operation x1, loops' own time, local(): sums_z = lax.map(along_z, sep_z)  33.2 us
    dynamic_slice x48, local copies, waits for them, and re-layouts, lag_sums(): return lax.map(one_lag, (leading, lag_values))  29.1 us
    reduce_sum x32, other arithmetic, one_lag(): return jnp.sum(head * tail)  24.8 us
    reduce_sum x16, other arithmetic, along_z(): return jnp.sum(w_field * shifted)  13.1 us
  transfers between devices with their start and end apart: 3, of which 0 were waited for; matrix products, arithmetic and copies ran while one was open for 27% of the time, Pallas kernels for 0%

profile of v1, /device:TPU:1, one launch (start us, length us, event | category | flops | bytes accessed | tf_op | source)
XLA Modules:
  0.0 308.3 jit_solution(1507923410366247618)
XLA Ops:
  0.0 3.3 %collective-permute-start = (f32[8,64,256]{2,1,0:T(8,128)}, f32[8,64,256]{2,1,0:T(8,128)S(1)}, u32[]{:S(2)}, u32[]{:S(2)}) collective-permute-start(f32[8,64,256]{2,1,0:T(8,128)} %param.12), channel_id=1, source_target_pairs={{0,31},{1,0},{2,1},{3,2},{4,3},{5,4},{6,5},{7,6},{8,7},{9,8},{10,9... | collective-permute-start | bytes 1572872 | tf_op jit(solution)/shard_map/ppermute | solution.py:21
  3.3 3.5 %collective-permute-start.2 = (f32[8,64,256]{2,1,0:T(8,128)}, f32[8,64,256]{2,1,0:T(8,128)S(1)}, u32[]{:S(2)}, u32[]{:S(2)}) collective-permute-start(f32[8,64,256]{2,1,0:T(8,128)} %param.13), channel_id=1, source_target_pairs={{0,224},{32,0},{64,32},{96,64},{128,96},{160,128},{192,160},{224,1... | collective-permute-start | bytes 1572872 | tf_op jit(solution)/shard_map/ppermute | solution.py:21
  6.8 1.8 multiply_reduce_fusion.5
  8.6 1.8 multiply_reduce_fusion.4
  10.4 1.9 multiply_reduce_fusion.3
  13.5 2.0 maximum_dynamic-update-slice_fusion
  15.6 6.5 %all-reduce.1 = f32[12]{0:T(128)S(1)} all-reduce(f32[12]{0:T(128)S(1)} %maximum_dynamic-update-slice_fusion), channel_id=7, replica_groups=mesh['gy_0'=4,'gy_1'=2,'gx_0'=2,'gx_1'=8,'gx_2'=2] {'gy_0'}, use_global_device_ids=true, to_apply=%add.1 | all-reduce | flops 12 | bytes 96
  23.7 5.3 %all-reduce.2 = f32[6]{0:T(128)S(1)} all-reduce(f32[6]{0:T(128)S(1)} %dynamic-update-slice.1), channel_id=8, replica_groups=mesh['gy_0'=4,'gy_1'=2,'gx_0'=2,'gx_1'=8,'gx_2'=2] {'gy_1'}, use_global_device_ids=true, to_apply=%add.2 | all-reduce | flops 6 | bytes 48
  30.5 3.8 %all-reduce.3 = f32[6]{0:T(128)S(1)} all-reduce(f32[6]{0:T(128)S(1)} %dynamic-update-slice.2), channel_id=9, replica_groups=mesh['gy_0'=4,'gy_1'=2,'gx_0'=2,'gx_1'=8,'gx_2'=2] {'gx_0'}, use_global_device_ids=true, to_apply=%add.3 | all-reduce | flops 6 | bytes 48
  35.9 16.7 %all-reduce.4 = f32[24]{0:T(128)S(1)} all-reduce(f32[24]{0:T(128)S(1)} %dynamic-update-slice.3), channel_id=10, replica_groups=mesh['gy_0'=4,'gy_1'=2,'gx_0'=2,'gx_1'=8,'gx_2'=2] {'gx_1'}, use_global_device_ids=true, to_apply=%add.4 | all-reduce | flops 24 | bytes 192
  54.3 69.7 %while.32 = (s32[]{:T(128)}, f32[16]{0:T(128)S(1)}, s32[16]{0:T(128)S(1)}, f32[16,64,256]{2,1,0:T(8,128)S(1)}, f32[8,64,256]{2,1,0:T(8,128)S(1)}, /*index=5*/s32[]{:T(128)}, s32[]{:T(128)}, s32[]{:T(128)}) while((s32[]{:T(128)}, f32[16]{0:T(128)S(1)}, s32[16]{0:T(128)S(1)}, f32[16,64,256]{2,1,0:T(8,128)S(1)}, f32[8,64,256]{2,1,0:T(8,128)S(1)}, ...), condition=%wide.region_8.9_spmd, body=%wide.region_6.8_spmd.sunk | while | flops 262148 | bytes 1048727 | solution.py:58
  57.1 0.8 multiply_reduce_fusion.11
  61.4 0.8 multiply_reduce_fusion.11
  65.8 0.8 multiply_reduce_fusion.11
  70.1 0.8 multiply_reduce_fusion.11
  74.5 0.8 multiply_reduce_fusion.11
  78.8 0.8 multiply_reduce_fusion.11
  83.2 0.8 multiply_reduce_fusion.11
  105.0 0.8 multiply_reduce_fusion.11
  109.3 0.8 multiply_reduce_fusion.11
  113.7 0.8 multiply_reduce_fusion.11
  118.0 0.8 multiply_reduce_fusion.11
  124.0 10.5 %all-reduce.5 = f32[6]{0:T(128)S(1)} all-reduce(f32[6]{0:T(128)S(1)} %dynamic-update-slice.4), channel_id=11, replica_groups=mesh['gy_0'=4,'gy_1'=2,'gx_0'=2,'gx_1'=8,'gx_2'=2] {'gx_2'}, use_global_device_ids=true, to_apply=%add.5 | all-reduce | flops 6 | bytes 48
  135.8 59.6 %while.31 = (s32[]{:T(128)}, f32[16]{0:T(128)S(1)}, f32[8,64,512]{2,1,0:T(8,128)S(1)}, s32[16]{0:T(128)S(1)}, s32[]{:T(128)}, /*index=5*/s32[]{:T(128)}, s32[]{:T(128)}) while((s32[]{:T(128)}, f32[16]{0:T(128)S(1)}, f32[8,64,512]{2,1,0:T(8,128)S(1)}, s32[16]{0:T(128)S(1)}, s32[]{:T(128)}, /*index=5*/s32[]{:T(128)}, s32[]{:T(128)}) %tuple.58), condition=%wide.region_5.6_spmd, body=%wide.region_3.5_spmd.sunk | while | flops 262148 | bytes 1048719 | solution.py:38
  195.4 1.2 pad_maximum_fusion
  196.6 64.5 %while.30 = (s32[]{:T(128)}, f32[16]{0:T(128)S(1)}, f32[8,192,256]{2,1,0:T(8,128)S(1)}, s32[16]{0:T(128)S(1)}, s32[]{:T(128)}, /*index=5*/s32[]{:T(128)}, s32[]{:T(128)}) while((s32[]{:T(128)}, f32[16]{0:T(128)S(1)}, f32[8,192,256]{2,1,0:T(8,128)S(1)}, s32[16]{0:T(128)S(1)}, s32[]{:T(128)}, /*index=5*/s32[]{:T(128)}, s32[]{:T(128)}) %tuple.59), condition=%wide.region_2.3_spmd, body=%wide.region_0.2_spmd.sunk | while | flops 262148 | bytes 1048719 | solution.py:38
  261.1 8.1 %all-gather.10 = f32[4,3,16]{2,1,0:T(4,128)S(1)} all-gather(f32[1,3,16]{2,1,0:T(4,128)S(1)} %maximum_bitcast_fusion), channel_id=2, replica_groups=mesh['gy_0'=4,'gy_1'=2,'gx_0'=2,'gx_1'=8,'gx_2'=2] {'gy_0'}, dimensions={0}, use_global_device_ids=true | all-gather | bytes 960 | tf_op jit(solution)/shard_map/all_gather | solution.py:13
  269.3 4.7 %all-gather.11 = f32[2,3,16]{2,1,0:T(4,128)S(1)} all-gather(f32[1,3,16]{2,1,0:T(4,128)S(1)} %bitcast.47), channel_id=3, replica_groups=mesh['gy_0'=4,'gy_1'=2,'gx_0'=2,'gx_1'=8,'gx_2'=2] {'gy_1'}, dimensions={0}, use_global_device_ids=true | all-gather | bytes 576 | tf_op jit(solution)/shard_map/all_gather | solution.py:13
  274.0 3.2 %all-gather.12 = f32[2,3,16]{2,1,0:T(4,128)S(1)} all-gather(f32[1,3,16]{2,1,0:T(4,128)S(1)} %bitcast.45), channel_id=4, replica_groups=mesh['gy_0'=4,'gy_1'=2,'gx_0'=2,'gx_1'=8,'gx_2'=2] {'gx_0'}, dimensions={0}, use_global_device_ids=true | all-gather | bytes 576 | tf_op jit(solution)/shard_map/all_gather | solution.py:13
  277.2 15.6 %all-gather.13 = f32[8,3,16]{2,1,0:T(4,128)S(1)} all-gather(f32[1,3,16]{2,1,0:T(4,128)S(1)} %bitcast.46), channel_id=5, replica_groups=mesh['gy_0'=4,'gy_1'=2,'gx_0'=2,'gx_1'=8,'gx_2'=2] {'gx_1'}, dimensions={0}, use_global_device_ids=true | all-gather | bytes 1728 | tf_op jit(solution)/shard_map/all_gather | solution.py:13
  292.8 13.0 %all-gather.14 = f32[2,3,16]{2,1,0:T(4,128)S(1)} all-gather(f32[1,3,16]{2,1,0:T(4,128)S(1)} %bitcast.44), channel_id=6, replica_groups=mesh['gy_0'=4,'gy_1'=2,'gx_0'=2,'gx_1'=8,'gx_2'=2] {'gx_2'}, dimensions={0}, use_global_device_ids=true | all-gather | bytes 576 | tf_op jit(solution)/shard_map/all_gather | solution.py:13
  306.4 1.3 slice_divide_fusion.1
  (197 shorter events, 100.5 us)
Async XLA Ops:
  0.0 12.3 %copy-start.10 = (u32[256]{0:T(256)S(1)}, u32[256]{0:T(256)}, u32[]{:S(2)}) copy-start(u32[256]{0:T(256)} %constant.46) | copy-start | bytes 3076
  0.0 22.2 %copy-start.9 = (u32[256]{0:T(256)S(1)}, u32[256]{0:T(256)}, u32[]{:S(2)}) copy-start(u32[256]{0:T(256)} %constant.51) | copy-start | bytes 3076
  0.0 29.0 %copy-start.8 = (u32[256]{0:T(256)S(1)}, u32[256]{0:T(256)}, u32[]{:S(2)}) copy-start(u32[256]{0:T(256)} %constant.56) | copy-start | bytes 3076
  0.0 34.4 %copy-start.7 = (u32[256]{0:T(256)S(1)}, u32[256]{0:T(256)}, u32[]{:S(2)}) copy-start(u32[256]{0:T(256)} %constant.61) | copy-start | bytes 3076
  0.0 52.7 %copy-start.6 = (u32[256]{0:T(256)S(1)}, u32[256]{0:T(256)}, u32[]{:S(2)}) copy-start(u32[256]{0:T(256)} %constant.66) | copy-start | bytes 3076
  0.0 53.9 %copy-start = (f32[8,64,256]{2,1,0:T(8,128)S(1)}, f32[8,64,256]{2,1,0:T(8,128)}, u32[]{:S(2)}) copy-start(f32[8,64,256]{2,1,0:T(8,128)} %param.14) | copy-start | bytes 1572868
  0.0 135.2 %collective-permute-start = (f32[8,64,256]{2,1,0:T(8,128)}, f32[8,64,256]{2,1,0:T(8,128)S(1)}, u32[]{:S(2)}, u32[]{:S(2)}) collective-permute-start(f32[8,64,256]{2,1,0:T(8,128)} %param.12), channel_id=1, source_target_pairs={{0,31},{1,0},{2,1},{3,2},{4,3},{5,4},{6,5},{7,6},{8,7},{9,8},{10,9... | collective-permute-start | bytes 1572872 | tf_op jit(solution)/shard_map/ppermute | solution.py:21
  3.3 132.3 %collective-permute-start.2 = (f32[8,64,256]{2,1,0:T(8,128)}, f32[8,64,256]{2,1,0:T(8,128)S(1)}, u32[]{:S(2)}, u32[]{:S(2)}) collective-permute-start(f32[8,64,256]{2,1,0:T(8,128)} %param.13), channel_id=1, source_target_pairs={{0,224},{32,0},{64,32},{96,64},{128,96},{160,128},{192,160},{224,1... | collective-permute-start | bytes 1572872 | tf_op jit(solution)/shard_map/ppermute | solution.py:21
  6.8 47.5 %copy-start.3 = (s32[16]{0:T(128)S(1)}, s32[16]{0:T(128)}, u32[]{:S(2)}) copy-start(s32[16]{0:T(128)} %param.17) | copy-start | bytes 196
  54.3 81.3 %copy-start.1 = (f32[8,64,256]{2,1,0:T(8,128)S(1)}, f32[8,64,256]{2,1,0:T(8,128)}, u32[]{:S(2)}) copy-start(f32[8,64,256]{2,1,0:T(8,128)} %param.13) | copy-start | bytes 1572868
  124.0 11.7 %copy-start.4 = (s32[16]{0:T(128)S(1)}, s32[16]{0:T(128)}, u32[]{:S(2)}) copy-start(s32[16]{0:T(128)} %param.16) | copy-start | bytes 196
  135.3 60.1 %collective-permute-start.1 = (f32[8,64,256]{2,1,0:T(8,128)S(1)}, f32[8,64,256]{2,1,0:T(8,128)}, u32[]{:S(2)}, u32[]{:S(2)}) collective-permute-start(f32[8,64,256]{2,1,0:T(8,128)S(1)} %collective-permute-done), channel_id=1, source_target_pairs={{0,31},{1,0},{2,1},{3,2},{4,3},{5,4},{6,5},{7,6},{8,7},{9,8},{10,9... | collective-permute-start | bytes 1572872 | tf_op jit(solution)/shard_map/ppermute | solution.py:21
  135.8 59.6 %copy-start.2 = (f32[8,64,256]{2,1,0:T(8,128)S(1)}, f32[8,64,256]{2,1,0:T(8,128)}, u32[]{:S(2)}) copy-start(f32[8,64,256]{2,1,0:T(8,128)} %param.12) | copy-start | bytes 1572868
  195.4 1.2 copy-start.5
